TPU v7x, 256 devices: a 2x2x32 block of a 4x8x32 slice. The times are simulated.
256 devices in a mesh: beam: 4 (over y, x), freq: 32 (over z), sub: 2 (over core).
Axes of the slice: x: 2, y: 2, z: 32, core: 2. Of those that a mesh axis runs over, the one named last changes fastest.
The devices are a block of a 4x8x32 slice.
Arguments:
- spectrum: bfloat16 [64, 4194304], P('sub', ('beam', 'freq')), parts along dimension 1
- hit_mask: int32 [64, 32768], P('sub', ('beam', 'freq')), parts along dimension 1, may hold values from 0 to 1, as said below
- owner_map: int32 [4096], P(('beam', 'freq')), parts along dimension 0, may hold values from 0 to 1023, as said below
- median_bin: int32 [4096], P(('beam', 'freq')), parts along dimension 0, may hold values from 32 to 559
- mad_bin: int32 [4096], P(('beam', 'freq')), parts along dimension 0, may hold values from 4 to 15
Outputs:
- hit_snr: bfloat16 [32, 2, 16384, 128], P('freq', 'sub', 'beam'), parts along dimension 2
- hit_keys: int32 [32, 2, 16384], P('freq', 'sub', 'beam'), parts along dimension 2
- hit_excess: float32 [32, 2, 16384], P('freq', 'sub', 'beam'), parts along dimension 2
There are 4 independent parts, one for each index of `beam`. A program takes and returns all parts, laid end to end along the dimension named above; each array names one. Nothing has to cross between parts.
Inputs may be any that keep to these rules, and one draw needn't show every extreme that they name: `hit_mask`: for each index of freq, each half of the drift rates and each owner, at most 128 hit blocks go from the first to the last; in every draw some owner gets exactly 128 from every index of freq and half. `owner_map`: A permutation of the slots 0 to 1023; the 32 coarse channels of one index of freq go 1 to each owner, and the slot of index f's coarse channel at each owner is f.
All inputs are finite; a program needn't handle non-finite values.
Results may differ from a plain program's by a relative error of at most 0.007.
Values may be sent and summed in bfloat16 or wider, within the bound.
A program may use at most 64 MiB of HBM per device.

v0:
```python
import jax
import jax.numpy as jnp
from jax import lax
from jax.sharding import PartitionSpec as P

COARSE_WIDTH = 1024
BLOCK = 128
CAP = 128


BIN_STEP = 0.0625
MAD_WIDTH = 5.0
MAD_SCALE = 1.4826
THRESH = 3.0


def copy_for_each(value, axis):
    devices = lax.axis_size(axis)
    return lax.all_to_all(
        jnp.broadcast_to(value[None], (devices, *value.shape)), axis, 0, 0, tiled=True
    )


def over_copies(value, axis):
    return copy_for_each(value, axis).sum(axis=0)


def together(arrays, axis):
    vector, at, done = (jnp.concatenate([a.reshape(-1) for a in arrays]), 0, [])
    subtotal = over_copies(vector, axis)
    for a in arrays:
        done.append(subtotal[at : at + a.size].reshape(a.shape))
        at += a.size
    return tuple(done)


def pick_from(selector, table):
    return jnp.sum(selector * table[None, :], axis=1)


def per_device(spectrum, hit_mask, owner_map, median_bin, mad_bin):
    drift_dev = spectrum.shape[0]
    coarse_dev = owner_map.shape[0]
    per_coarse = COARSE_WIDTH // BLOCK
    freq_count = lax.axis_size("freq")
    drift_total = drift_dev * lax.axis_size("sub")
    half_index = lax.axis_index("sub")
    slots_total = freq_count * CAP
    power = spectrum.astype(jnp.float32).reshape(drift_dev, coarse_dev, COARSE_WIDTH)
    center = BIN_STEP * median_bin.astype(jnp.float32)
    spread = MAD_WIDTH * BIN_STEP * mad_bin.astype(jnp.float32)
    inside = (power >= (center - spread)[None, :, None]) & (
        power <= (center + spread)[None, :, None]
    )
    kept = jnp.where(inside, power - center[None, :, None], 0.0)
    window_count = jnp.sum(inside.astype(jnp.float32), axis=(0, 2))
    first = jnp.sum(kept, axis=(0, 2))
    second = jnp.sum(kept * kept, axis=(0, 2))
    window_count, first, second = together((window_count, first, second), "sub")
    floor_count = jnp.maximum(window_count, 1.0)
    mean_level = center + first / floor_count
    mad_sigma = MAD_SCALE * BIN_STEP * mad_bin.astype(jnp.float32)
    sigma = jnp.sqrt(0.5 * second / floor_count + 0.5 * mad_sigma * mad_sigma)
    marks = hit_mask.reshape(drift_dev, coarse_dev, per_coarse)
    row_count = jnp.sum(marks, axis=2)
    coarse_count = jnp.sum(row_count, axis=0)
    row_start = jnp.cumsum(row_count, axis=0) - row_count
    dest = owner_map // coarse_dev
    slot_local = owner_map % coarse_dev
    ahead = ((dest[None, :] == dest[:, None]) & (slot_local[None, :] < slot_local[:, None])).astype(
        jnp.int32
    )
    offset = jnp.sum(ahead * coarse_count[None, :], axis=1)
    positions = jnp.arange(slots_total, dtype=jnp.int32)
    target_dest = positions // CAP
    within = positions % CAP
    select = (
        (dest[None, :] == target_dest[:, None])
        & (offset[None, :] <= within[:, None])
        & (within[:, None] < (offset + coarse_count)[None, :])
    )
    filled = jnp.any(select, axis=1)
    pick = select.astype(jnp.int32)
    coarse_ids = jnp.arange(coarse_dev, dtype=jnp.int32)
    chosen_coarse = pick_from(pick, coarse_ids)
    chosen_slot = pick_from(pick, slot_local)
    remain = within - pick_from(pick, offset)
    pick_float = pick.astype(jnp.float32)
    starts_at = jnp.dot(
        pick_float, row_start.T.astype(jnp.float32), precision=lax.Precision.HIGHEST
    ).astype(jnp.int32)
    counts_at = jnp.dot(
        pick_float, row_count.T.astype(jnp.float32), precision=lax.Precision.HIGHEST
    ).astype(jnp.int32)
    row_pick = ((starts_at <= remain[:, None]) & (remain[:, None] < starts_at + counts_at)).astype(
        jnp.int32
    )
    chosen_drift = pick_from(row_pick, jnp.arange(drift_dev, dtype=jnp.int32))
    inner = remain - jnp.sum(row_pick * starts_at, axis=1)
    bit_rows = marks.reshape(-1, per_coarse)[chosen_drift * coarse_dev + chosen_coarse]
    bit_before = jnp.cumsum(bit_rows, axis=1) - bit_rows
    bit_pick = ((bit_rows > 0) & (bit_before == inner[:, None])).astype(jnp.int32)
    chosen_block = pick_from(bit_pick, jnp.arange(per_coarse, dtype=jnp.int32))
    source_row = jnp.where(
        filled, (chosen_drift * coarse_dev + chosen_coarse) * per_coarse + chosen_block, 0
    )
    slot_keys = jnp.where(
        filled,
        (chosen_slot * drift_total + half_index * drift_dev + chosen_drift) * per_coarse
        + chosen_block,
        -1,
    )
    blocks = spectrum.reshape(-1, BLOCK)[source_row]
    level = jnp.sum(pick_float * mean_level[None, :], axis=1)
    scale = jnp.where(filled, jnp.sum(pick_float * sigma[None, :], axis=1), 1.0)
    normal = (blocks.astype(jnp.float32) - level[:, None]) / scale[:, None]
    payload = jnp.where(filled[:, None], normal, 0.0).astype(jnp.bfloat16)
    arrived = lax.all_to_all(
        payload.reshape(freq_count, CAP, BLOCK), "freq", split_axis=0, concat_axis=0, tiled=True
    )
    keys = lax.all_to_all(
        slot_keys.reshape(freq_count, CAP), "freq", split_axis=0, concat_axis=0, tiled=True
    )
    excess = jnp.sum(jnp.maximum(arrived.astype(jnp.float32) - THRESH, 0.0), axis=-1)
    hit_rows, arrived_keys, excess = (arrived, keys, excess)
    got = jnp.sum((arrived_keys >= 0).astype(jnp.int32), axis=1)
    ends = jnp.cumsum(got)
    begins = ends - got
    source_of = jnp.sum((ends[None, :] <= positions[:, None]).astype(jnp.int32), axis=1)
    live = source_of < freq_count
    source_clip = jnp.minimum(source_of, freq_count - 1)
    source_hot = (jnp.arange(freq_count, dtype=jnp.int32)[None, :] == source_clip[:, None]).astype(
        jnp.int32
    )
    begin_of = jnp.sum(source_hot * begins[None, :], axis=1)
    take = jnp.where(live, source_clip * CAP + positions - begin_of, 0)
    hit_snr = jnp.where(
        live[:, None], hit_rows.reshape(-1, BLOCK)[take], jnp.zeros((1, BLOCK), jnp.bfloat16)
    )
    hit_keys = jnp.where(live, arrived_keys.reshape(-1)[take], -1).astype(jnp.int32)
    hit_excess = jnp.where(live, excess.reshape(-1)[take], 0.0)
    return (
        hit_snr.reshape(1, 1, slots_total, BLOCK),
        hit_keys.reshape(1, 1, slots_total),
        hit_excess.reshape(1, 1, slots_total),
    )


def solution(mesh):
    placed = (
        P("sub", ("beam", "freq")),
        P("sub", ("beam", "freq")),
        P(("beam", "freq")),
        P(("beam", "freq")),
        P(("beam", "freq")),
    )
    return jax.shard_map(
        per_device,
        mesh=mesh,
        in_specs=placed,
        out_specs=(
            P("freq", "sub", "beam", None),
            P("freq", "sub", "beam"),
            P("freq", "sub", "beam"),
        ),
        check_vma=False,
    )
```

profile of v0, /device:TPU:37, one launch (start us, length us, event | category | flops | bytes accessed | tf_op | source)
XLA Modules:
  0.0 246.7 jit_solution(17346366266765123883)
XLA Ops:
  0.6 0.7 fusion.28
  1.3 0.1 broadcast_bitcast_fusion.2
  1.4 0.1 broadcast_bitcast_fusion
  1.6 0.0 copy-start
  1.6 0.0 copy-start.3
  1.6 0.0 copy-start.1
  1.6 0.0 copy-start.2
  1.6 3.6 %fusion.5 = (f32[32768]{0:T(1024)S(1)}, f32[32768]{0:T(1024)S(1)}, f32[32768]{0:T(1024)S(1)}) fusion(bf16[32,32768]{1,0:T(8,128)(2,1)} %param.5, f32[32768]{0:T(1024)S(1)} %bitcast.42, f32[32768]{0:T(1024)S(1)} %bitcast.43, f32[32768]{0:T(1024)S(1)} %bitcast.41), kind=kLoop, calls=%fused_computation.15 | loop fusion | flops 11436032 | bytes 2883584 | tf_op jit(solution)/shard_map/reduce_sum | solution.py:57
  5.3 0.1 reduce_sum.227
  5.5 0.1 reduce_sum.230
  5.6 0.1 reduce_sum.224
  5.7 0.1 pad_maximum_fusion
  5.8 0.6 broadcast_in_dim.49
  6.4 23.6 %all-to-all-start.1 = ((f32[2,1,96]{2,1,0:T(1,128)}), f32[2,1,96]{2,1,0:T(1,128)S(1)}, u32[]{:S(2)}, u32[]{:S(2)}) async-start(f32[2,1,96]{2,1,0:T(1,128)} %broadcast_in_dim.49), calls=%async_computation.1 | async-start | bytes 2048 | tf_op jit(solution)/shard_map/all_to_all | solution.py:19
  30.0 0.0 copy-done
  30.0 0.1 copy.25
  30.1 0.0 copy-done.3
  30.1 0.1 reduce_sum.208
  30.2 0.1 reduce_sum.209
  30.4 0.2 select_reduce_fusion.7
  30.6 0.4 all-to-all-done.1
  31.0 0.0 copy-done.1
  31.0 0.0 copy-done.2
  31.0 0.1 add_sqrt_fusion
  31.1 0.3 multiply_reduce_fusion.1
  31.4 0.3 select_reduce_fusion.6
  31.7 0.1 copy.35
  31.7 0.3 reshape_reshape.3
  32.1 0.1 copy.26
  32.2 0.1 reduce_window_sum.29
  32.2 0.6 convolution_convert_fusion.1
  32.9 0.8 select_reduce_fusion.2
  33.8 10.8 %gather_fusion = s32[4096,8]{1,0:T(8,128)S(1)} fusion(s32[1024,8]{1,0:T(8,128)S(1)} %reshape_reshape.3, s32[4096]{0:T(1024)S(1)} %broadcast_clamp_fusion.2), kind=kCustom, calls=%fused_computation | custom fusion | bytes 278528 | tf_op jit(solution)/shard_map/gather | solution.py:100
  44.5 2.4 reduce_window_sum.30
  47.0 0.1 reduce_or.13
  47.1 2.5 %select_reduce_fusion = s32[4096]{0:T(1024)S(1)} fusion(s32[4096,8]{1,0:T(8,128)} %reduce_window_sum.30, s32[4096,8]{1,0:T(8,128)S(1)} %gather_fusion, s32[4096]{0:T(1024)S(1)} %fusion.29), kind=kLoop, calls=%fused_computation.24 | loop fusion | flops 192512 | bytes 294912 | tf_op jit(solution)/shard_map/reduce_sum | solution.py:38
  49.6 0.6 add_select_fusion.1
  50.2 13.4 %all-to-all-start = ((s32[32,1,128]{2,1,0:T(1,128)}), s32[32,1,128]{2,1,0:T(1,128)S(1)}, u32[]{:S(2)}, u32[]{:S(2)}) async-start(s32[32,1,128]{2,1,0:T(1,128)} %bitcast.3), calls=%async_computation | async-start | bytes 32768 | tf_op jit(solution)/shard_map/all_to_all | solution.py:121
  63.6 2.9 %reshape.382 = bf16[8192,128]{1,0:T(8,128)(2,1)S(1)} reshape(bf16[32,32768]{1,0:T(8,128)(2,1)} %param.5) | data formatting | bytes 4194304 | tf_op jit(solution)/shard_map/reshape | solution.py:113
  66.6 12.1 %gather_fusion.1 = bf16[4096,128]{1,0:T(8,128)(2,1)S(1)} fusion(bf16[8192,128]{1,0:T(8,128)(2,1)S(1)} %reshape.382, s32[4096]{0:T(1024)S(1)} %broadcast_clamp_fusion.1), kind=kCustom, calls=%fused_computation.1 | custom fusion | bytes 2113536 | tf_op jit(solution)/shard_map/gather | solution.py:113
  78.7 2.9 %fusion.10 = bf16[32,128,128]{2,1,0:T(8,128)(2,1)} fusion(bf16[32,128,128]{2,1,0:T(8,128)(2,1)S(1)} %bitcast.40, f32[32,128]{1,0:T(8,128)S(1)} %bitcast_select_fusion.1, f32[32,128]{1,0:T(8,128)S(1)} %bitcast.48, pred[32,128]{1,0:T(8,128)(4,1)S(1)} %bitcast.47), kind=kLoop, calls=%fused_computation.22 | loop fusion | flops 2621440 | bytes 2134016 | tf_op jit(solution)/shard_map/convert_element_type | solution.py:117
  81.5 2.6 %all-to-all-done = s32[32,1,128]{2,1,0:T(1,128)S(1)} async-done(((s32[32,1,128]{2,1,0:T(1,128)}), s32[32,1,128]{2,1,0:T(1,128)S(1)}, u32[]{:S(2)}, u32[]{:S(2)}) %all-to-all-start) | async-done | bytes 16416 | tf_op jit(solution)/shard_map/all_to_all | solution.py:121
  84.1 19.1 %all-to-all-start.2 = ((bf16[32,128,128]{2,1,0:T(8,128)(2,1)}), bf16[32,128,128]{2,1,0:T(8,128)(2,1)S(1)}, u32[]{:S(2)}, u32[]{:S(2)}) async-start(bf16[32,128,128]{2,1,0:T(8,128)(2,1)} %fusion.10), calls=%async_computation.2 | async-start | bytes 2097152 | tf_op jit(solution)/shard_map/all_to_all | solution.py:118
  103.2 0.1 convert_reduce_fusion.2
  103.3 0.1 copy.29
  103.4 0.1 reduce-window.7
  103.5 0.1 reduce.11
  103.6 0.1 convert_reduce_fusion.1
  103.8 0.2 select_reduce_fusion.1
  104.0 23.0 %gather_fusion.3 = s32[4096]{0:T(1024)S(1)} fusion(s32[4096]{0:T(1024)S(1)} %bitcast.37, s32[4096]{0:T(1024)S(1)} %broadcast_clamp_fusion), kind=kCustom, calls=%fused_computation.3 | custom fusion | bytes 49152 | tf_op jit(solution)/shard_map/gather | solution.py:140
  127.0 0.6 broadcast_select_fusion.1
  127.6 79.8 %all-to-all-done.2 = bf16[32,128,128]{2,1,0:T(8,128)(2,1)S(1)} async-done(((bf16[32,128,128]{2,1,0:T(8,128)(2,1)}), bf16[32,128,128]{2,1,0:T(8,128)(2,1)S(1)}, u32[]{:S(2)}, u32[]{:S(2)}) %all-to-all-start.2) | async-done | bytes 1048608 | tf_op jit(solution)/shard_map/all_to_all | solution.py:118
  207.4 0.6 maximum_reduce_fusion
  208.0 23.0 %gather_fusion.4 = f32[4096]{0:T(1024)S(1)} fusion(f32[4096]{0:T(1024)S(1)} %bitcast.38, s32[4096]{0:T(1024)S(1)} %broadcast_clamp_fusion), kind=kCustom, calls=%fused_computation.4 | custom fusion | bytes 49152 | tf_op jit(solution)/shard_map/gather | solution.py:141
  231.1 12.1 %gather_fusion.2 = bf16[4096,128]{1,0:T(8,128)(2,1)S(1)} fusion(bf16[4096,128]{1,0:T(8,128)(2,1)S(1)} %bitcast.39, s32[4096]{0:T(1024)S(1)} %broadcast_clamp_fusion), kind=kCustom, calls=%fused_computation.2 | custom fusion | bytes 2113536 | tf_op jit(solution)/shard_map/gather | solution.py:138
  243.2 0.6 broadcast_select_fusion
  243.8 2.9 %bitcast_select_fusion = bf16[1,1,4096,128]{3,2,1,0:T(8,128)(2,1)} fusion(bf16[4096,128]{1,0:T(8,128)(2,1)S(1)} %gather_fusion.2, pred[4096]{0:T(1024)(128)(4,1)S(1)} %broadcast_compare_fusion), kind=kLoop, calls=%fused_computation.27 | loop fusion | flops 524288 | bytes 2101248 | tf_op jit(solution)/shard_map/jit(_where)/select_n | solution.py:137
  (25 shorter events, 0.4 us)
Async XLA Ops:
  1.6 28.4 %copy-start = (s32[32,256]{1,0:T(8,128)S(1)}, s32[32,256]{1,0:T(8,128)}, u32[]{:S(2)}) copy-start(s32[32,256]{1,0:T(8,128)} %param.6) | copy-start | bytes 98308
  1.6 28.5 %copy-start.3 = (s32[32]{0:T(128)S(1)}, s32[32]{0:T(128)}, u32[]{:S(2)}) copy-start(s32[32]{0:T(128)} %param.7) | copy-start | bytes 388
  1.6 29.4 %copy-start.1 = (s32[32]{0:T(128)S(1)}, s32[32]{0:T(128)}, u32[]{:S(2)}) copy-start(s32[32]{0:T(128)} %param.9) | copy-start | bytes 388
  1.6 29.4 %copy-start.2 = (s32[32]{0:T(128)S(1)}, s32[32]{0:T(128)}, u32[]{:S(2)}) copy-start(s32[32]{0:T(128)} %param.8) | copy-start | bytes 388
  6.4 24.6 %all-to-all-start.1 = ((f32[2,1,96]{2,1,0:T(1,128)}), f32[2,1,96]{2,1,0:T(1,128)S(1)}, u32[]{:S(2)}, u32[]{:S(2)}) async-start(f32[2,1,96]{2,1,0:T(1,128)} %broadcast_in_dim.49), calls=%async_computation.1 | async-start | bytes 2048 | tf_op jit(solution)/shard_map/all_to_all | solution.py:19
  50.2 34.0 %all-to-all-start = ((s32[32,1,128]{2,1,0:T(1,128)}), s32[32,1,128]{2,1,0:T(1,128)S(1)}, u32[]{:S(2)}, u32[]{:S(2)}) async-start(s32[32,1,128]{2,1,0:T(1,128)} %bitcast.3), calls=%async_computation | async-start | bytes 32768 | tf_op jit(solution)/shard_map/all_to_all | solution.py:121
  84.1 123.3 %all-to-all-start.2 = ((bf16[32,128,128]{2,1,0:T(8,128)(2,1)}), bf16[32,128,128]{2,1,0:T(8,128)(2,1)S(1)}, u32[]{:S(2)}, u32[]{:S(2)}) async-start(bf16[32,128,128]{2,1,0:T(8,128)(2,1)} %fusion.10), calls=%async_computation.2 | async-start | bytes 2097152 | tf_op jit(solution)/shard_map/all_to_all | solution.py:118
where the time goes:
time: 247 us
  local copies, waits for them, and re-layouts  85.6 us (35%)
  waiting for transfers between devices  82.8 us (34%)
  starting transfers between devices  56.1 us (23%)
  other arithmetic  19.8 us (8%)
    all_to_all x1, waiting for transfers between devices, per_device(): lax.all_to_all(payload.reshape(freq_count, CAP, BLOCK), 'freq', split_axi...  79.8 us
    all_to_all x1, starting transfers between devices, copy_for_each(): lax.all_to_all(jnp.broadcast_to(value[None], (devices, *value.shape)), ax...  23.6 us
    gather x1, local copies, waits for them, and re-layouts, per_device(): arrived_keys.reshape(-1)[take]  23 us
    gather x1, local copies, waits for them, and re-layouts, per_device(): hit_excess = jnp.where(live, excess.reshape(-1)[take], 0.0)  23 us
    all_to_all x1, starting transfers between devices, per_device(): lax.all_to_all(payload.reshape(freq_count, CAP, BLOCK), 'freq', split_axi...  19.1 us
    all_to_all x1, starting transfers between devices, per_device(): lax.all_to_all(slot_keys.reshape(freq_count, CAP), 'freq', split_axis=0,...  13.4 us
    gather x1, local copies, waits for them, and re-layouts, per_device(): blocks = spectrum.reshape(-1, BLOCK)[source_row]  12.1 us
    gather x1, local copies, waits for them, and re-layouts, per_device(): hit_rows.reshape(-1, BLOCK)[take]  12.1 us
  transfers between devices with their start and end apart: 3, of which 3 were waited for; matrix products, arithmetic and copies ran while one was open for 17% of the time, Pallas kernels for 0%

commit v1 on v0

v1 whole, which is shorter than its diff:
```python
import functools

import jax
import jax.numpy as jnp
from jax import lax
from jax.experimental import pallas as pl
from jax.experimental.pallas import tpu as pltpu
from jax.sharding import PartitionSpec as P

COARSE_WIDTH = 1024
BLOCK = 128
CAP = 128
PER = COARSE_WIDTH // BLOCK

BIN_STEP = 0.0625
MAD_WIDTH = 5.0
MAD_SCALE = 1.4826
THRESH = 3.0

VMEM = pltpu.VMEM
SMEM = pltpu.SMEM
MESH = pl.DeviceIdType.MESH
F32 = jnp.float32
BF16 = jnp.bfloat16


def dot_nt(a, b):
    return lax.dot_general(a, b, (((1,), (1,)), ((), ())), preferred_element_type=F32)


def stats_kernel(coarse, low, high, mid, spec, center, mad, mean_out, sigma_out, mine, theirs, sems):
    other = 1 - lax.axis_index("sub")
    barrier = pltpu.get_barrier_semaphore()
    pl.semaphore_signal(barrier, inc=1, device_id={"sub": other}, device_id_type=MESH)

    def one(c, carry):
        lo, hi, at = low[c], high[c], mid[c]
        count = first = second = None
        for b in range(PER):
            x = spec[:, pl.ds(pl.multiple_of(c * COARSE_WIDTH + b * BLOCK, BLOCK), BLOCK)].astype(F32)
            inside = (x >= lo) & (x <= hi)
            kept = jnp.where(inside, x - at, 0.0)
            ones = jnp.where(inside, 1.0, 0.0)
            square = kept * kept
            count = ones if b == 0 else count + ones
            first = kept if b == 0 else first + kept
            second = square if b == 0 else second + square
        mine[0, pl.ds(c, 1), :] = jnp.sum(count, axis=0, keepdims=True)
        mine[1, pl.ds(c, 1), :] = jnp.sum(first, axis=0, keepdims=True)
        mine[2, pl.ds(c, 1), :] = jnp.sum(second, axis=0, keepdims=True)
        return carry

    lax.fori_loop(0, coarse, one, 0, unroll=2)
    pl.semaphore_wait(barrier, 1)
    copy = pltpu.make_async_remote_copy(
        src_ref=mine, dst_ref=theirs, send_sem=sems.at[0], recv_sem=sems.at[1],
        device_id={"sub": other}, device_id_type=MESH,
    )
    copy.start()
    copy.wait()
    total = [jnp.sum(mine[k] + theirs[k], axis=1, keepdims=True) for k in range(3)]
    floor = jnp.maximum(total[0], 1.0)
    mean = center[...] + total[1] / floor
    mad_sigma = MAD_SCALE * BIN_STEP * mad[...]
    sigma = jnp.sqrt(0.5 * total[2] / floor + 0.5 * mad_sigma * mad_sigma)
    mean_out[...] = jnp.broadcast_to(mean, mean_out.shape)
    sigma_out[...] = jnp.broadcast_to(sigma, sigma_out.shape)


def displacement(i, n):
    step = n // 2 - i // 2
    return jnp.where(i == 0, 0, jnp.where(i % 2 == 1, step, n - step))


def exchange_kernel(
    n, drift, total_drift, source_of, spec, marks, mean, sigma,
    rows, keys, excess, begins,
    rank, filled, send_rows, send_codes, got_codes, row_sems, code_sems,
):
    me = lax.axis_index("freq")
    half = lax.axis_index("sub")
    barrier = pltpu.get_barrier_semaphore()

    def greet(i, carry):
        pl.semaphore_signal(barrier, inc=1, device_id={"freq": (me + i) % n}, device_id_type=MESH)
        return carry

    lax.fori_loop(1, n, greet, 0)
    width = PER * drift

    def position(at):
        tile, block, row = at // (PER * 8), at // 8 % PER, at % 8
        return (tile * 8 + row) * PER + block

    def order(axis):
        return position(lax.broadcasted_iota(jnp.int32, (width, width), axis))

    before = jnp.where(order(0) < order(1), 1.0, 0.0).astype(BF16)
    set_here = marks[...]
    mark_float = set_here.astype(F32)
    ranks = jnp.dot(mark_float.astype(BF16), before, preferred_element_type=F32)
    rank[...] = jnp.where(set_here > 0, ranks, -1.0)
    filled[...] = jnp.broadcast_to(jnp.sum(mark_float, axis=1, keepdims=True), filled.shape)
    at = lax.broadcasted_iota(jnp.int32, (8, width), 1)
    code = (position(at) + 1).astype(F32).astype(BF16)
    slot_wide = lax.broadcasted_iota(jnp.int32, (CAP, width), 0).astype(F32)
    slot = lax.broadcasted_iota(jnp.int32, (CAP, BLOCK), 0).astype(F32)

    def build(owner):
        c = source_of[owner]
        chosen = jnp.where(slot_wide == rank[pl.ds(c, 1), :], 1.0, 0.0).astype(BF16)
        blocks = spec[:, pl.ds(c * PER, PER)].reshape(width, BLOCK)
        power = jnp.dot(chosen, blocks, preferred_element_type=F32)
        normal = (power - mean[pl.ds(c, 1), :]) / sigma[pl.ds(c, 1), :]
        payload = jnp.where(slot < filled[pl.ds(c, 1), :], normal, 0.0).astype(BF16)
        return payload, dot_nt(code, chosen)[0:1]

    payload, codes = build(me)
    rows[me] = payload
    got_codes[me] = codes

    def pack(i, carry):
        payload, codes = build((me + displacement(i, n)) % n)
        send_rows[i] = payload
        send_codes[i] = codes
        return carry

    lax.fori_loop(1, n, pack, 0, unroll=2)

    def code_copy(i):
        return pltpu.make_async_remote_copy(
            src_ref=send_codes.at[i], dst_ref=got_codes.at[me],
            send_sem=code_sems.at[0, i], recv_sem=code_sems.at[1, i],
            device_id={"freq": (me + displacement(i, n)) % n}, device_id_type=MESH,
        )

    def row_copy(i):
        return pltpu.make_async_remote_copy(
            src_ref=send_rows.at[i], dst_ref=rows.at[me],
            send_sem=row_sems.at[0, i], recv_sem=row_sems.at[1, i],
            device_id={"freq": (me + displacement(i, n)) % n}, device_id_type=MESH,
        )

    pl.semaphore_wait(barrier, n - 1)

    def start_codes(i, carry):
        code_copy(i).start()
        return carry

    def start_rows(i, carry):
        row_copy(i).start()
        return carry

    lax.fori_loop(1, n, start_codes, 0)
    lax.fori_loop(1, n, start_rows, 0)
    ones = jnp.ones((8, BLOCK), BF16)

    def take_codes(sender):
        codes = got_codes[sender]
        base = (sender * total_drift + half * drift) * PER - 1
        keys[pl.ds(sender, 1), :] = jnp.where(codes > 0, codes + base.astype(F32), -1.0)

    def take_rows(sender):
        over = jnp.maximum(rows[sender].astype(F32) - THRESH, 0.0)
        coarse_part = over.astype(BF16)
        fine_part = (over - coarse_part.astype(F32)).astype(BF16)
        excess[pl.ds(sender, 1), :] = (dot_nt(ones, coarse_part) + dot_nt(ones, fine_part))[0:1]

    take_codes(me)
    take_rows(me)

    def codes_in(i, carry):
        code_copy(i).wait()
        take_codes((me + n - displacement(i, n)) % n)
        return carry

    def rows_in(i, carry):
        row_copy(i).wait()
        take_rows((me + n - displacement(i, n)) % n)
        return carry

    lax.fori_loop(1, n, codes_in, 0)
    live = jnp.where(keys[...] >= 0, 1.0, 0.0).astype(BF16)
    counts = dot_nt(ones, live)
    earlier = jnp.where(
        lax.broadcasted_iota(jnp.int32, (n, n), 0) < lax.broadcasted_iota(jnp.int32, (n, n), 1), 1.0, 0.0
    ).astype(BF16)
    begins[...] = jnp.dot(counts.astype(BF16), earlier, preferred_element_type=F32).astype(jnp.int32)
    lax.fori_loop(1, n, rows_in, 0)


def compact_kernel(n, begins, rows, keys, excess, snr_out, keys_out, excess_out, wide, key_rows, excess_rows):
    wide[...] = jnp.zeros_like(wide)
    key_rows[...] = jnp.full_like(key_rows, -1.0)
    excess_rows[...] = jnp.zeros_like(excess_rows)
    lane = lax.broadcasted_iota(jnp.int32, (1, BLOCK), 1)
    for s in range(n):
        begin = begins[0, s]
        wide[pl.ds(begin, CAP), :] = rows[s].astype(F32)
        row, shift = begin // BLOCK, begin % BLOCK
        for source, target, empty in ((keys, key_rows, -1.0), (excess, excess_rows, 0.0)):
            turned = pltpu.roll(source[pl.ds(s, 1), :], shift, 1)
            here, after = pl.ds(row, 1), pl.ds(row + 1, 1)
            target[here, :] = jnp.where(lane >= shift, turned, target[here, :])
            target[after, :] = jnp.where(lane < shift, turned, empty)
    snr_out[...] = wide[...].astype(BF16)
    keys_out[...] = key_rows[0:n, :].astype(jnp.int32)
    excess_out[...] = excess_rows[0:n, :]


def per_device(spectrum, hit_mask, owner_map, median_bin, mad_bin):
    drift = spectrum.shape[0]
    coarse = owner_map.shape[0]
    n = lax.axis_size("freq")
    total_drift = drift * lax.axis_size("sub")
    width = PER * drift
    center = BIN_STEP * median_bin.astype(F32)
    mad = mad_bin.astype(F32)
    spread = MAD_WIDTH * BIN_STEP * mad
    vmem, smem = pl.BlockSpec(memory_space=VMEM), pl.BlockSpec(memory_space=SMEM)
    mean, sigma = pl.pallas_call(
        functools.partial(stats_kernel, coarse),
        out_shape=[jax.ShapeDtypeStruct((coarse, BLOCK), F32)] * 2,
        in_specs=[smem] * 3 + [vmem] * 3,
        out_specs=[vmem] * 2,
        scratch_shapes=[
            VMEM((3, coarse, BLOCK), F32), VMEM((3, coarse, BLOCK), F32), pltpu.SemaphoreType.DMA((2,)),
        ],
        compiler_params=pltpu.CompilerParams(collective_id=1, has_side_effects=True),
        name="stats",
    )(center - spread, center + spread, center, spectrum, center[:, None], mad[:, None])
    tiles = spectrum.reshape(drift // 8, 8, coarse * PER, BLOCK).transpose(0, 2, 1, 3)
    marks = hit_mask.reshape(drift // 8, 8, coarse, PER).transpose(2, 0, 3, 1).reshape(coarse, width)
    dest = owner_map // coarse
    owners = jnp.arange(n, dtype=jnp.int32)
    source_of = jnp.sum(
        jnp.where(dest[None, :] == owners[:, None], jnp.arange(coarse, dtype=jnp.int32)[None, :], 0), axis=1
    )
    rows, keys, excess, begins = pl.pallas_call(
        functools.partial(exchange_kernel, n, drift, total_drift),
        out_shape=[
            jax.ShapeDtypeStruct((n, CAP, BLOCK), BF16),
            jax.ShapeDtypeStruct((n, BLOCK), F32),
            jax.ShapeDtypeStruct((n, BLOCK), F32),
            jax.ShapeDtypeStruct((8, n), jnp.int32),
        ],
        in_specs=[smem] + [vmem] * 4,
        out_specs=[vmem] * 4,
        scratch_shapes=[
            VMEM((coarse, width), F32), VMEM((coarse, BLOCK), F32),
            VMEM((n, CAP, BLOCK), BF16), VMEM((n, 1, CAP), F32), VMEM((n, 1, CAP), F32),
            pltpu.SemaphoreType.DMA((2, n)), pltpu.SemaphoreType.DMA((2, n)),
        ],
        compiler_params=pltpu.CompilerParams(collective_id=0, has_side_effects=True),
        name="exchange",
    )(source_of, tiles, marks, mean, sigma)
    snr, keys, excess = pl.pallas_call(
        functools.partial(compact_kernel, n),
        out_shape=[
            jax.ShapeDtypeStruct((n * CAP, BLOCK), BF16),
            jax.ShapeDtypeStruct((n, BLOCK), jnp.int32),
            jax.ShapeDtypeStruct((n, BLOCK), F32),
        ],
        in_specs=[smem] + [vmem] * 3,
        out_specs=[vmem] * 3,
        scratch_shapes=[VMEM((n * CAP, BLOCK), F32), VMEM((n + 8, BLOCK), F32), VMEM((n + 8, BLOCK), F32)],
        name="compact",
    )(begins, rows, keys, excess)
    total = n * CAP
    return snr.reshape(1, 1, total, BLOCK), keys.reshape(1, 1, total), excess.reshape(1, 1, total)


def solution(mesh):
    placed = (
        P("sub", ("beam", "freq")),
        P("sub", ("beam", "freq")),
        P(("beam", "freq")),
        P(("beam", "freq")),
        P(("beam", "freq")),
    )
    return jax.shard_map(
        per_device,
        mesh=mesh,
        in_specs=placed,
        out_specs=(
            P("freq", "sub", "beam", None),
            P("freq", "sub", "beam"),
            P("freq", "sub", "beam"),
        ),
        check_vma=False,
    )
```

time: 247 us -> 144 us (0.58)
  Pallas kernels: 0 us -> 137 us
  local copies, waits for them, and re-layouts: 85.6 us -> 2.59 us
  waiting for transfers between devices: 82.8 us -> 0 us
  starting transfers between devices: 56.1 us -> 0 us
  other arithmetic: 19.8 us -> 3.28 us
    pallas_call x0 -> x3, Pallas kernels: none -> 137 us  [the longest x1 108 us: per_device(): pl.pallas_call(functools.partial(exchange_kernel, n, drift, total_drift),...]
    all_to_all x3 -> x0, waiting for transfers between devices: 82.8 us -> none  [the longest x1 79.8 us: per_device(): lax.all_to_all(payload.reshape(freq_count, CAP, BLOCK), 'freq', split_axi...]
    gather x5 -> x0, local copies, waits for them, and re-layouts: 81.1 us -> none  [the longest x1 23 us: per_device(): arrived_keys.reshape(-1)[take]]
    all_to_all x3 -> x0, starting transfers between devices: 56.1 us -> none  [the longest x1 23.6 us: copy_for_each(): lax.all_to_all(jnp.broadcast_to(value[None], (devices, *value.shape)), ax...]
    reduce_sum x16 -> x1, other arithmetic: 8.49 us -> 0.69 us  [per_device(): jnp.sum(jnp.where(dest[None, :] == owners[:, None], jnp.arange(coarse, dt...]
    select_n x10 -> x1, other arithmetic: 4.82 us -> 0.67 us  [per_device(): dest = owner_map // coarse]
    convert_element_type x1 -> x0, other arithmetic: 2.85 us -> none  [per_device(): payload = jnp.where(filled[:, None], normal, 0.0).astype(jnp.bfloat16)]
    another operation x4 -> x0, other arithmetic: 2.67 us -> none  [the longest x1 2.44 us: per_device(): bit_before = jnp.cumsum(bit_rows, axis=1) - bit_rows]
  transfers between devices with their start and end apart: 3 -> 0, of which waited for: 3 -> 0; matrix products, arithmetic and copies ran while one was open for 17% -> 0% of each run, Pallas kernels for 0% -> 0%
where the time goes in v1:
time: 144 us; the launch traced here: 143 us
  Pallas kernels  137 us (95%)
  other arithmetic  3.28 us (2%)
  local copies, waits for them, and re-layouts  2.59 us (2%)
    pallas_call x1, Pallas kernels, per_device(): pl.pallas_call(functools.partial(exchange_kernel, n, drift, total_drift),...  108 us
    pallas_call x1, Pallas kernels, per_device(): pl.pallas_call(functools.partial(stats_kernel, coarse), out_shape=[jax.Sh...  25.5 us

profile of v1, /device:TPU:37, one launch (start us, length us, event | category | flops | bytes accessed | tf_op | source)
XLA Modules:
  0.0 143.3 jit_solution(12342950704935868204)
XLA Ops:
  0.6 0.0 copy-start
  0.6 0.7 and_select_fusion
  1.3 0.7 select_reduce_fusion.source_of
  2.0 0.7 convert_bitcast_fusion
  2.7 1.3 fusion
  3.9 0.7 copy.17.mad
  4.6 0.7 copy.16.center
  5.3 25.5 %stats.1 = (f32[32,128]{1,0:T(8,128)}, f32[32,128]{1,0:T(8,128)}) custom-call(f32[32]{0:T(128)} %get-tuple-element.22.low, f32[32]{0:T(128)} %get-tuple-element.21.high, f32[32]{0:T(128)} %get-tuple-element.24.mid, bf16[32,32768]{1,0:T(8,128)(2,1)} %spec.1, f32[32,1]{1,0:T(8,128)} %copy.16.center, f32[32,1]{1,0:T(8,128)} %copy.17.mad), custom_call_target="tpu_custom_call" | custom-call | tf_op jit(solution)/shard_map/stats/pallas_call | solution.py:221
  30.8 0.0 copy-done
  30.8 0.3 reshape.26
  31.1 0.2 copy.15
  31.3 0.7 copy.18.marks
  32.0 108.4 %exchange.1 = (bf16[32,128,128]{2,1,0:T(8,128)(2,1)}, f32[32,128]{1,0:T(8,128)}, f32[32,128]{1,0:T(8,128)}, s32[8,32]{1,0:T(8,128)}) custom-call(s32[32]{0:T(128)} %select_reduce_fusion.source_of, bf16[4,256,8,128]{3,2,1,0:T(8,128)(2,1)} %bitcast.12, s32[32,256]{1,0:T(8,128)} %copy.18.marks, f32[32,128]{1,0:T(8,128)} %get-tuple-element.12.mean, ...), custom_call_target="tpu_custom_call" | custom-call | tf_op jit(solution)/shard_map/exchange/pallas_call | solution.py:239
  140.5 2.8 %compact.1 = (bf16[4096,128]{1,0:T(8,128)(2,1)}, s32[32,128]{1,0:T(8,128)}, f32[32,128]{1,0:T(8,128)}) custom-call(s32[8,32]{1,0:T(8,128)} %get-tuple-element.14.begins, bf16[32,128,128]{2,1,0:T(8,128)(2,1)} %get-tuple-element.15.rows, f32[32,128]{1,0:T(8,128)} %get-tuple-element.16.keys, f32[32,128]{1,0:T(8,128)} %get-tuple-element.17.excess), custom_call_target="tpu_custom_call" | custom-call | tf_op jit(solution)/shard_map/compact/pallas_call | solution.py:257
Async XLA Ops:
  0.6 30.2 %copy-start = (s32[32,256]{1,0:T(8,128)S(1)}, s32[32,256]{1,0:T(8,128)}, u32[]{:S(2)}) copy-start(s32[32,256]{1,0:T(8,128)} %param.6) | copy-start | bytes 98308

commit v2 on v1

v2 whole, which is shorter than its diff:
```python
import functools

import jax
import jax.numpy as jnp
from jax import lax
from jax.experimental import pallas as pl
from jax.experimental.pallas import tpu as pltpu
from jax.sharding import PartitionSpec as P

COARSE_WIDTH = 1024
BLOCK = 128
CAP = 128
PER = COARSE_WIDTH // BLOCK

BIN_STEP = 0.0625
MAD_WIDTH = 5.0
MAD_SCALE = 1.4826
THRESH = 3.0

VMEM = pltpu.VMEM
SMEM = pltpu.SMEM
MESH = pl.DeviceIdType.MESH
F32 = jnp.float32
BF16 = jnp.bfloat16


def dot_nt(a, b):
    return lax.dot_general(a, b, (((1,), (1,)), ((), ())), preferred_element_type=F32)


REACH = 4


def exchange_kernel(
    n, coarse, drift, total_drift,
    owner_hbm, median_hbm, mad_hbm, marks_hbm, spec_hbm,
    rows, keys, excess, begins,
    owner, median, mad, source_of, marks, spec, mine, theirs, mean, sigma, rank, filled,
    send_rows, send_codes, got_codes,
    small_sems, spec_sems, stat_sems, row_sems, code_sems, chain,
):
    me = lax.axis_index("freq")
    half = lax.axis_index("sub")
    far = n // 2
    rounds = far // REACH - 1
    groups = spec_sems.shape[0]
    group = coarse // groups
    width = PER * drift
    barrier = pltpu.get_barrier_semaphore()
    small = [
        pltpu.make_async_copy(src, dst, small_sems.at[k])
        for k, (src, dst) in enumerate(
            ((owner_hbm, owner), (median_hbm, median), (mad_hbm, mad), (marks_hbm, marks))
        )
    ]
    large = []
    for g in range(groups):
        part = pl.ds(g * group * PER, group * PER)
        large.append(pltpu.make_async_copy(spec_hbm.at[:, part], spec.at[:, part], spec_sems.at[g]))
    for copy in small + large:
        copy.start()
    pl.semaphore_signal(barrier, inc=1, device_id={"sub": 1 - half}, device_id_type=MESH)
    for d in range(1, REACH + 1):
        for to in (me + d, me + n - d):
            pl.semaphore_signal(barrier, inc=1, device_id={"freq": to % n}, device_id_type=MESH)

    for copy in small:
        copy.wait()

    def position(at):
        tile, block, row = at // (PER * 8), at // 8 % PER, at % 8
        return (tile * 8 + row) * PER + block

    def iota(shape, axis):
        return lax.broadcasted_iota(jnp.int32, shape, axis)

    def hot(mask):
        return jnp.where(mask, 1.0, 0.0).astype(BF16)

    lanes = coarse * PER
    spread = hot(iota((lanes, lanes), 1) == iota((lanes, lanes), 0) % coarse * PER + iota((lanes, lanes), 0) // coarse)
    by_block = dot_nt(spread, marks[...].astype(F32).astype(BF16)).astype(BF16)
    ranks = set_here = None
    for b in range(PER):
        here = by_block[b * coarse : (b + 1) * coarse]
        come, go = iota((drift, width), 0) * PER + b, position(iota((drift, width), 1))
        before = jnp.dot(here, hot(come < go), preferred_element_type=F32)
        same = jnp.dot(here, hot(come == go), preferred_element_type=F32)
        ranks = before if b == 0 else ranks + before
        set_here = same if b == 0 else set_here + same
    rank[...] = jnp.where(set_here > 0, ranks, -1.0)
    filled[...] = jnp.broadcast_to(jnp.sum(set_here, axis=1, keepdims=True), filled.shape)

    def stats(c, carry):
        center = BIN_STEP * median[c].astype(F32)
        deviation = mad[c].astype(F32)
        wide = MAD_WIDTH * BIN_STEP * deviation
        mean[pl.ds(c, 1), :] = jnp.full((1, BLOCK), center, F32)
        sigma[pl.ds(c, 1), :] = jnp.full((1, BLOCK), MAD_SCALE * BIN_STEP * deviation, F32)
        found = 0
        for k in range(coarse):
            found = jnp.where(owner[k] == c * coarse + me, k, found)
        source_of[c] = found
        x = spec[:, pl.ds(c * PER, PER)].astype(F32)
        inside = (x >= center - wide) & (x <= center + wide)
        kept = jnp.where(inside, x - center, 0.0)
        for k, each in enumerate((jnp.where(inside, 1.0, 0.0), kept, kept * kept)):
            mine[k, pl.ds(c, 1), :] = jnp.sum(jnp.sum(each, axis=(0, 1)), axis=0, keepdims=True)
        return carry

    for g in range(groups):
        large[g].wait()
        lax.fori_loop(g * group, (g + 1) * group, stats, 0)

    pl.semaphore_wait(barrier, 2 * REACH + 1)

    def tell(k):
        for to in (me + REACH, me + n - REACH):
            pl.semaphore_signal(chain.at[k], inc=1, device_id={"freq": to % n}, device_id_type=MESH)

    share = pltpu.make_async_remote_copy(
        src_ref=mine, dst_ref=theirs, send_sem=stat_sems.at[0], recv_sem=stat_sems.at[1],
        device_id={"sub": 1 - half}, device_id_type=MESH,
    )
    share.start()
    if rounds:
        tell(0)

    def hear(k):
        if k < rounds:
            pl.semaphore_wait(chain.at[k], 2)
            if k + 1 < rounds:
                tell(k + 1)

    at = iota((8, width), 1)
    code = (position(at) + 1).astype(F32).astype(BF16)
    slot_wide = iota((CAP, width), 0).astype(F32)
    slot = iota((CAP, BLOCK), 0).astype(F32)
    share.wait()
    total = [jnp.sum(mine[k] + theirs[k], axis=1, keepdims=True) for k in range(3)]
    floor = jnp.maximum(total[0], 1.0)
    mean[...] = mean[...] + total[1] / floor
    sigma[...] = jnp.sqrt(0.5 * total[2] / floor + 0.5 * sigma[...] * sigma[...])

    def build(to):
        c = source_of[to]
        chosen = hot(slot_wide == rank[pl.ds(c, 1), :])
        blocks = spec[:, pl.ds(c * PER, PER)].reshape(width, BLOCK)
        power = jnp.dot(chosen, blocks, preferred_element_type=F32)
        normal = (power - mean[pl.ds(c, 1), :]) / sigma[pl.ds(c, 1), :]
        payload = jnp.where(slot < filled[pl.ds(c, 1), :], normal, 0.0).astype(BF16)
        return payload, dot_nt(code, chosen)[0:1]

    def pack(d):
        payload, codes = build((me + d) % n)
        send_rows[d] = payload
        send_codes[d] = codes

    def code_copy(d):
        return pltpu.make_async_remote_copy(
            src_ref=send_codes.at[d], dst_ref=got_codes.at[me],
            send_sem=code_sems.at[0, d], recv_sem=code_sems.at[1, d],
            device_id={"freq": (me + d) % n}, device_id_type=MESH,
        )

    def row_copy(d):
        return pltpu.make_async_remote_copy(
            src_ref=send_rows.at[d], dst_ref=rows.at[me],
            send_sem=row_sems.at[0, d], recv_sem=row_sems.at[1, d],
            device_id={"freq": (me + d) % n}, device_id_type=MESH,
        )

    def send(d):
        code_copy(d).start()
        row_copy(d).start()

    def each(first, last, act):
        def body(k, carry):
            m = first - k
            act(m)
            act(n - m)
            return carry
        lax.fori_loop(0, first - last + 1, body, 0)

    def pack_send(ms):
        waiting = []
        for d in [d for m in ms for d in (m, n - m)]:
            pack(d)
            if waiting:
                send(waiting.pop())
            waiting.append(d)
        send(waiting.pop())

    early = [m for m in (2, 4, 3) if m <= REACH and m < far]
    middle = [m for m in (6,) if REACH < m <= 2 * REACH and m < far]
    near = [m for m in range(2 * REACH, 0, -1) if m not in early + middle and m < far]
    top = far - 1
    deep = max(top - 3, 2 * REACH + 1)
    pack_send(early)
    hear(0)
    if middle:
        pack_send(middle)
    if far > 2 * REACH:
        pack(far)
        each(top, deep, pack)
        hear(1)
        if deep > 2 * REACH + 1:
            each(deep - 1, 2 * REACH + 1, pack)
        for k in range(2, rounds):
            hear(k)
        send(far)
        each(top, 2 * REACH + 1, send)
    else:
        pack(far)
        send(far)
    if near:
        pack_send(near)

    ones = jnp.ones((8, BLOCK), BF16)

    def take(sender):
        codes = got_codes[sender]
        base = (sender * total_drift + half * drift) * PER - 1
        keys[pl.ds(sender, 1), :] = jnp.where(codes > 0, codes + base.astype(F32), -1.0)
        over = jnp.maximum(rows[sender].astype(F32) - THRESH, 0.0)
        coarse_part = over.astype(BF16)
        fine_part = (over - coarse_part.astype(F32)).astype(BF16)
        excess[pl.ds(sender, 1), :] = (dot_nt(ones, coarse_part) + dot_nt(ones, fine_part))[0:1]

    def arrive(d):
        code_copy(d).wait()
        row_copy(d).wait()
        take((me + n - d) % n)

    payload, codes = build(me)
    rows[me] = payload
    got_codes[me] = codes
    take(me)
    for m in early + middle:
        arrive(m)
        arrive(n - m)
    arrive(far)
    if far > 2 * REACH:
        each(top, 2 * REACH + 1, arrive)
    for m in near:
        arrive(m)
        arrive(n - m)
    counts = dot_nt(ones, hot(keys[...] >= 0))
    earlier = hot(iota((n, n), 0) < iota((n, n), 1))
    begins[...] = jnp.dot(counts.astype(BF16), earlier, preferred_element_type=F32).astype(jnp.int32)


def compact_kernel(n, begins, rows, keys, excess, snr_out, keys_out, excess_out, wide, key_rows, excess_rows):
    wide[...] = jnp.zeros_like(wide)
    key_rows[...] = jnp.full_like(key_rows, -1.0)
    excess_rows[...] = jnp.zeros_like(excess_rows)
    lane = lax.broadcasted_iota(jnp.int32, (1, BLOCK), 1)
    for s in range(n):
        begin = begins[0, s]
        wide[pl.ds(begin, CAP), :] = rows[s].astype(F32)
        row, shift = begin // BLOCK, begin % BLOCK
        for source, target, empty in ((keys, key_rows, -1.0), (excess, excess_rows, 0.0)):
            turned = pltpu.roll(source[pl.ds(s, 1), :], shift, 1)
            here, after = pl.ds(row, 1), pl.ds(row + 1, 1)
            target[here, :] = jnp.where(lane >= shift, turned, target[here, :])
            target[after, :] = jnp.where(lane < shift, turned, empty)
    snr_out[...] = wide[...].astype(BF16)
    keys_out[...] = key_rows[0:n, :].astype(jnp.int32)
    excess_out[...] = excess_rows[0:n, :]


def per_device(spectrum, hit_mask, owner_map, median_bin, mad_bin):
    drift = spectrum.shape[0]
    coarse = owner_map.shape[0]
    n = lax.axis_size("freq")
    total_drift = drift * lax.axis_size("sub")
    width = PER * drift
    vmem, smem = pl.BlockSpec(memory_space=VMEM), pl.BlockSpec(memory_space=SMEM)
    tiles = spectrum.reshape(drift // 8, 8, coarse * PER, BLOCK).transpose(0, 2, 1, 3)
    table = VMEM((coarse, BLOCK), F32)
    dma = pltpu.SemaphoreType.DMA
    rows, keys, excess, begins = pl.pallas_call(
        functools.partial(exchange_kernel, n, coarse, drift, total_drift),
        out_shape=[
            jax.ShapeDtypeStruct((n, CAP, BLOCK), BF16),
            jax.ShapeDtypeStruct((n, BLOCK), F32),
            jax.ShapeDtypeStruct((n, BLOCK), F32),
            jax.ShapeDtypeStruct((8, n), jnp.int32),
        ],
        in_specs=[pl.BlockSpec(memory_space=pl.ANY)] * 5,
        out_specs=[vmem] * 4,
        scratch_shapes=[
            SMEM((coarse,), jnp.int32), SMEM((coarse,), jnp.int32), SMEM((coarse,), jnp.int32),
            SMEM((coarse,), jnp.int32),
            VMEM(hit_mask.shape, jnp.int32), VMEM(tiles.shape, BF16),
            VMEM((3, coarse, BLOCK), F32), VMEM((3, coarse, BLOCK), F32), table, table,
            VMEM((coarse, width), F32), table,
            VMEM((n, CAP, BLOCK), BF16), VMEM((n, 1, CAP), F32), VMEM((n, 1, CAP), F32),
            dma((4,)), dma((4,)), dma((2,)), dma((2, n)), dma((2, n)),
            pltpu.SemaphoreType.REGULAR((max(n // 2 // REACH - 1, 1),)),
        ],
        compiler_params=pltpu.CompilerParams(collective_id=0, has_side_effects=True),
        name="exchange",
    )(owner_map, median_bin, mad_bin, hit_mask, tiles)
    snr, keys, excess = pl.pallas_call(
        functools.partial(compact_kernel, n),
        out_shape=[
            jax.ShapeDtypeStruct((n * CAP, BLOCK), BF16),
            jax.ShapeDtypeStruct((n, BLOCK), jnp.int32),
            jax.ShapeDtypeStruct((n, BLOCK), F32),
        ],
        in_specs=[smem] + [vmem] * 3,
        out_specs=[vmem] * 3,
        scratch_shapes=[VMEM((n * CAP, BLOCK), F32), VMEM((n + 8, BLOCK), F32), VMEM((n + 8, BLOCK), F32)],
        name="compact",
    )(begins, rows, keys, excess)
    total = n * CAP
    return snr.reshape(1, 1, total, BLOCK), keys.reshape(1, 1, total), excess.reshape(1, 1, total)


def solution(mesh):
    placed = (
        P("sub", ("beam", "freq")),
        P("sub", ("beam", "freq")),
        P(("beam", "freq")),
        P(("beam", "freq")),
        P(("beam", "freq")),
    )
    return jax.shard_map(
        per_device,
        mesh=mesh,
        in_specs=placed,
        out_specs=(
            P("freq", "sub", "beam", None),
            P("freq", "sub", "beam"),
            P("freq", "sub", "beam"),
        ),
        check_vma=False,
    )
```

time: 144 us -> 129 us (0.90)
  Pallas kernels: 137 us -> 128 us
  other arithmetic: 3.28 us -> 0 us
  local copies, waits for them, and re-layouts: 2.59 us -> 0 us
    pallas_call x2 -> x1, Pallas kernels: 134 us -> 125 us  [per_device(): pl.pallas_call(functools.partial(exchange_kernel, n, coarse, drift, total...]
where the time goes in v2:
time: 129 us; the launch traced here: 128 us
  Pallas kernels  128 us (99%)
    pallas_call x1, Pallas kernels, per_device(): pl.pallas_call(functools.partial(exchange_kernel, n, coarse, drift, total...  125 us
    pallas_call x1, Pallas kernels, per_device(): pl.pallas_call(functools.partial(compact_kernel, n), out_shape=[jax.Shape...  2.79 us

profile of v2, /device:TPU:37, one launch (start us, length us, event | category | flops | bytes accessed | tf_op | source)
XLA Modules:
  0.0 128.3 jit_solution(13470362445415440582)
XLA Ops:
  0.6 124.9 %exchange.1 = (bf16[32,128,128]{2,1,0:T(8,128)(2,1)}, f32[32,128]{1,0:T(8,128)}, f32[32,128]{1,0:T(8,128)}, s32[8,32]{1,0:T(8,128)}) custom-call(s32[32]{0:T(128)} %owner_hbm.1, s32[32]{0:T(128)} %median_hbm.1, s32[32]{0:T(128)} %mad_hbm.1, s32[32,256]{1,0:T(8,128)} %marks_hbm.1, bf16[4,256,8,128]{3,2,1,0:T(8,128)(2,1)} %bitcast.6), custom_call_target="tpu_custom_call" | custom-call | tf_op jit(solution)/shard_map/exchange/pallas_call | solution.py:282
  125.5 2.8 %compact.1 = (bf16[4096,128]{1,0:T(8,128)(2,1)}, s32[32,128]{1,0:T(8,128)}, f32[32,128]{1,0:T(8,128)}) custom-call(s32[8,32]{1,0:T(8,128)} %get-tuple-element.10.begins, bf16[32,128,128]{2,1,0:T(8,128)(2,1)} %get-tuple-element.11.rows, f32[32,128]{1,0:T(8,128)} %get-tuple-element.12.keys, f32[32,128]{1,0:T(8,128)} %get-tuple-element.13.excess), custom_call_target="tpu_custom_call" | custom-call | tf_op jit(solution)/shard_map/compact/pallas_call | solution.py:305

commit v3 on v2

--- a/solution.py
+++ b/solution.py
@@ -36,8 +36,8 @@
     owner_hbm, median_hbm, mad_hbm, marks_hbm, spec_hbm,
     rows, keys, excess, begins,
     owner, median, mad, source_of, marks, spec, mine, theirs, mean, sigma, rank, filled,
-    send_rows, send_codes, got_codes,
-    small_sems, spec_sems, stat_sems, row_sems, code_sems, chain,
+    send_rows, send_codes, got_codes, send_norms, got_norms,
+    small_sems, spec_sems, stat_sems, row_sems, code_sems, norm_sems, chain,
 ):
     me = lax.axis_index("freq")
     half = lax.axis_index("sub")
@@ -91,6 +91,91 @@
     rank[...] = jnp.where(set_here > 0, ranks, -1.0)
     filled[...] = jnp.broadcast_to(jnp.sum(set_here, axis=1, keepdims=True), filled.shape)
 
+    early = [m for m in (2, 4, 3) if m <= REACH and m < far]
+    middle = [m for m in (6,) if REACH < m <= 2 * REACH and m < far]
+    late = [m for m in range(far - 1, 0, -1) if m not in early + middle]
+    run = next((k for k in range(1, len(late)) if late[k] != late[0] - k), len(late))
+
+    def ways(ms):
+        return [d for m in ms for d in (m, n - m)]
+
+    at = iota((8, width), 1)
+    code = (position(at) + 1).astype(F32).astype(BF16)
+    slot_wide = iota((CAP, width), 0).astype(F32)
+    slot = iota((CAP, BLOCK), 0).astype(F32)
+    lane = iota((1, BLOCK), 1)
+
+    def choose(c):
+        chosen = hot(slot_wide == rank[pl.ds(c, 1), :])
+        blocks = spec[:, pl.ds(c * PER, PER)].reshape(width, BLOCK)
+        return jnp.dot(chosen, blocks, preferred_element_type=F32), dot_nt(code, chosen)[0:1]
+
+    def build(c):
+        power, codes = choose(c)
+        normal = (power - mean[pl.ds(c, 1), :]) / sigma[pl.ds(c, 1), :]
+        return jnp.where(slot < filled[pl.ds(c, 1), :], normal, 0.0).astype(BF16), codes
+
+    def pack(d):
+        payload, codes = build(source_of[(me + d) % n])
+        send_rows[d] = payload
+        send_codes[d] = codes
+
+    def copies(send_buffer, buffer, sems):
+        def copy(d):
+            return pltpu.make_async_remote_copy(
+                src_ref=send_buffer.at[d], dst_ref=buffer.at[me],
+                send_sem=sems.at[0, d], recv_sem=sems.at[1, d],
+                device_id={"freq": (me + d) % n}, device_id_type=MESH,
+            )
+        return copy
+
+    row_copy = copies(send_rows, rows, row_sems)
+    code_copy = copies(send_codes, got_codes, code_sems)
+    norm_copy = copies(send_norms, got_norms, norm_sems)
+
+    def send(d):
+        code_copy(d).start()
+        row_copy(d).start()
+
+    def each_late(act):
+        def body(k, carry):
+            act(late[0] - k)
+            act(n - late[0] + k)
+            return carry
+        act(far)
+        if late:
+            lax.fori_loop(0, run, body, 0)
+        for d in ways(late[run:]):
+            act(d)
+
+    def tell(k):
+        if k < rounds:
+            for to in (me + REACH, me + n - REACH):
+                pl.semaphore_signal(chain.at[k], inc=1, device_id={"freq": to % n}, device_id_type=MESH)
+
+    def hear(k):
+        if k < rounds:
+            pl.semaphore_wait(chain.at[k], 2)
+            tell(k + 1)
+
+    owned = [owner[k] for k in range(coarse)]
+    sources = []
+    for d in ways(early):
+        wanted, found = (me + d) % n * coarse + me, 0
+        for k in range(coarse):
+            found = jnp.where(owned[k] == wanted, k, found)
+        sources.append(found)
+    for copy in large:
+        copy.wait()
+    for d, c in zip(ways(early), sources):
+        power, codes = choose(c)
+        send_rows[d] = power.astype(BF16)
+        send_codes[d] = codes
+    pl.semaphore_wait(barrier, 2 * REACH + 1)
+    tell(0)
+    for d in ways(early):
+        send(d)
+
     def stats(c, carry):
         center = BIN_STEP * median[c].astype(F32)
         deviation = mad[c].astype(F32)
@@ -108,146 +193,80 @@
             mine[k, pl.ds(c, 1), :] = jnp.sum(jnp.sum(each, axis=(0, 1)), axis=0, keepdims=True)
         return carry
 
-    for g in range(groups):
-        large[g].wait()
-        lax.fori_loop(g * group, (g + 1) * group, stats, 0)
-
-    pl.semaphore_wait(barrier, 2 * REACH + 1)
-
-    def tell(k):
-        for to in (me + REACH, me + n - REACH):
-            pl.semaphore_signal(chain.at[k], inc=1, device_id={"freq": to % n}, device_id_type=MESH)
-
+    lax.fori_loop(0, coarse, stats, 0, unroll=2)
+    hear(0)
     share = pltpu.make_async_remote_copy(
         src_ref=mine, dst_ref=theirs, send_sem=stat_sems.at[0], recv_sem=stat_sems.at[1],
         device_id={"sub": 1 - half}, device_id_type=MESH,
     )
     share.start()
-    if rounds:
-        tell(0)
-
-    def hear(k):
-        if k < rounds:
-            pl.semaphore_wait(chain.at[k], 2)
-            if k + 1 < rounds:
-                tell(k + 1)
-
-    at = iota((8, width), 1)
-    code = (position(at) + 1).astype(F32).astype(BF16)
-    slot_wide = iota((CAP, width), 0).astype(F32)
-    slot = iota((CAP, BLOCK), 0).astype(F32)
     share.wait()
     total = [jnp.sum(mine[k] + theirs[k], axis=1, keepdims=True) for k in range(3)]
     floor = jnp.maximum(total[0], 1.0)
     mean[...] = mean[...] + total[1] / floor
     sigma[...] = jnp.sqrt(0.5 * total[2] / floor + 0.5 * sigma[...] * sigma[...])
-
-    def build(to):
-        c = source_of[to]
-        chosen = hot(slot_wide == rank[pl.ds(c, 1), :])
-        blocks = spec[:, pl.ds(c * PER, PER)].reshape(width, BLOCK)
-        power = jnp.dot(chosen, blocks, preferred_element_type=F32)
-        normal = (power - mean[pl.ds(c, 1), :]) / sigma[pl.ds(c, 1), :]
-        payload = jnp.where(slot < filled[pl.ds(c, 1), :], normal, 0.0).astype(BF16)
-        return payload, dot_nt(code, chosen)[0:1]
-
-    def pack(d):
-        payload, codes = build((me + d) % n)
-        send_rows[d] = payload
-        send_codes[d] = codes
-
-    def code_copy(d):
-        return pltpu.make_async_remote_copy(
-            src_ref=send_codes.at[d], dst_ref=got_codes.at[me],
-            send_sem=code_sems.at[0, d], recv_sem=code_sems.at[1, d],
-            device_id={"freq": (me + d) % n}, device_id_type=MESH,
-        )
-
-    def row_copy(d):
-        return pltpu.make_async_remote_copy(
-            src_ref=send_rows.at[d], dst_ref=rows.at[me],
-            send_sem=row_sems.at[0, d], recv_sem=row_sems.at[1, d],
-            device_id={"freq": (me + d) % n}, device_id_type=MESH,
-        )
-
-    def send(d):
-        code_copy(d).start()
-        row_copy(d).start()
-
-    def each(first, last, act):
-        def body(k, carry):
-            m = first - k
-            act(m)
-            act(n - m)
-            return carry
-        lax.fori_loop(0, first - last + 1, body, 0)
-
-    def pack_send(ms):
-        waiting = []
-        for d in [d for m in ms for d in (m, n - m)]:
-            pack(d)
-            if waiting:
-                send(waiting.pop())
-            waiting.append(d)
-        send(waiting.pop())
-
-    early = [m for m in (2, 4, 3) if m <= REACH and m < far]
-    middle = [m for m in (6,) if REACH < m <= 2 * REACH and m < far]
-    near = [m for m in range(2 * REACH, 0, -1) if m not in early + middle and m < far]
-    top = far - 1
-    deep = max(top - 3, 2 * REACH + 1)
-    pack_send(early)
-    hear(0)
-    if middle:
-        pack_send(middle)
-    if far > 2 * REACH:
-        pack(far)
-        each(top, deep, pack)
-        hear(1)
-        if deep > 2 * REACH + 1:
-            each(deep - 1, 2 * REACH + 1, pack)
-        for k in range(2, rounds):
-            hear(k)
-        send(far)
-        each(top, 2 * REACH + 1, send)
-    else:
-        pack(far)
-        send(far)
-    if near:
-        pack_send(near)
+    for d, c in zip(ways(early), sources):
+        send_norms[d] = jnp.where(lane < BLOCK // 2, mean[pl.ds(c, 1), :], sigma[pl.ds(c, 1), :])
+    for d in ways(middle):
+        pack(d)
+    for d in ways(early):
+        norm_copy(d).start()
+    for d in ways(middle):
+        send(d)
+    hear(1)
+    each_late(pack)
+    for k in range(2, rounds):
+        hear(k)
+    each_late(lambda d: code_copy(d).start())
+    each_late(lambda d: row_copy(d).start())
 
     ones = jnp.ones((8, BLOCK), BF16)
 
-    def take(sender):
-        codes = got_codes[sender]
-        base = (sender * total_drift + half * drift) * PER - 1
-        keys[pl.ds(sender, 1), :] = jnp.where(codes > 0, codes + base.astype(F32), -1.0)
-        over = jnp.maximum(rows[sender].astype(F32) - THRESH, 0.0)
+    def sender(d):
+        return (me + n - d) % n
+
+    def take_codes(s):
+        codes = got_codes[s]
+        base = (s * total_drift + half * drift) * PER - 1
+        keys[pl.ds(s, 1), :] = jnp.where(codes > 0, codes + base.astype(F32), -1.0)
+
+    def take_rows(s):
+        over = jnp.maximum(rows[s].astype(F32) - THRESH, 0.0)
         coarse_part = over.astype(BF16)
         fine_part = (over - coarse_part.astype(F32)).astype(BF16)
-        excess[pl.ds(sender, 1), :] = (dot_nt(ones, coarse_part) + dot_nt(ones, fine_part))[0:1]
-
-    def arrive(d):
+        excess[pl.ds(s, 1), :] = (dot_nt(ones, coarse_part) + dot_nt(ones, fine_part))[0:1]
+
+    def codes_in(d):
         code_copy(d).wait()
+        take_codes(sender(d))
+
+    def rows_in(d):
         row_copy(d).wait()
-        take((me + n - d) % n)
-
-    payload, codes = build(me)
+        take_rows(sender(d))
+
+    payload, codes = build(source_of[me])
     rows[me] = payload
     got_codes[me] = codes
-    take(me)
-    for m in early + middle:
-        arrive(m)
-        arrive(n - m)
-    arrive(far)
-    if far > 2 * REACH:
-        each(top, 2 * REACH + 1, arrive)
-    for m in near:
-        arrive(m)
-        arrive(n - m)
+    take_codes(me)
+    take_rows(me)
+    for d in ways(early):
+        s = sender(d)
+        codes_in(d)
+        row_copy(d).wait()
+        norm_copy(d).wait()
+        live = jnp.sum(jnp.where(got_codes[s] > 0, 1.0, 0.0), axis=1, keepdims=True)
+        norms = got_norms[s]
+        normal = (rows[s].astype(F32) - norms[:, 0:1]) / norms[:, BLOCK // 2 : BLOCK // 2 + 1]
+        rows[s] = jnp.where(slot < live, normal, 0.0).astype(BF16)
+        take_rows(s)
+    for d in ways(middle):
+        codes_in(d)
+        rows_in(d)
+    each_late(codes_in)
     counts = dot_nt(ones, hot(keys[...] >= 0))
     earlier = hot(iota((n, n), 0) < iota((n, n), 1))
     begins[...] = jnp.dot(counts.astype(BF16), earlier, preferred_element_type=F32).astype(jnp.int32)
+    each_late(rows_in)
 
 
 def compact_kernel(n, begins, rows, keys, excess, snr_out, keys_out, excess_out, wide, key_rows, excess_rows):
@@ -277,7 +296,7 @@
     width = PER * drift
     vmem, smem = pl.BlockSpec(memory_space=VMEM), pl.BlockSpec(memory_space=SMEM)
     tiles = spectrum.reshape(drift // 8, 8, coarse * PER, BLOCK).transpose(0, 2, 1, 3)
-    table = VMEM((coarse, BLOCK), F32)
+    table, line = VMEM((coarse, BLOCK), F32), VMEM((n, 1, CAP), F32)
     dma = pltpu.SemaphoreType.DMA
     rows, keys, excess, begins = pl.pallas_call(
         functools.partial(exchange_kernel, n, coarse, drift, total_drift),
@@ -287,7 +306,7 @@
             jax.ShapeDtypeStruct((n, BLOCK), F32),
             jax.ShapeDtypeStruct((8, n), jnp.int32),
         ],
-        in_specs=[pl.BlockSpec(memory_space=pl.ANY)] * 5,
+        in_specs=[pl.BlockSpec(memory_space=pltpu.HBM)] * 5,
         out_specs=[vmem] * 4,
         scratch_shapes=[
             SMEM((coarse,), jnp.int32), SMEM((coarse,), jnp.int32), SMEM((coarse,), jnp.int32),
@@ -295,13 +314,15 @@
             VMEM(hit_mask.shape, jnp.int32), VMEM(tiles.shape, BF16),
             VMEM((3, coarse, BLOCK), F32), VMEM((3, coarse, BLOCK), F32), table, table,
             VMEM((coarse, width), F32), table,
-            VMEM((n, CAP, BLOCK), BF16), VMEM((n, 1, CAP), F32), VMEM((n, 1, CAP), F32),
-            dma((4,)), dma((4,)), dma((2,)), dma((2, n)), dma((2, n)),
+            VMEM((n, CAP, BLOCK), BF16), line, line, line, line,
+            dma((4,)), dma((4,)), dma((2,)), dma((2, n)), dma((2, n)), dma((2, n)),
             pltpu.SemaphoreType.REGULAR((max(n // 2 // REACH - 1, 1),)),
         ],
-        compiler_params=pltpu.CompilerParams(collective_id=0, has_side_effects=True),
+        compiler_params=pltpu.CompilerParams(
+            collective_id=0, has_side_effects=True, vmem_limit_bytes=16 * 1024 * 1024
+        ),
         name="exchange",
-    )(owner_map, median_bin, mad_bin, hit_mask, tiles)
+    )(*(pltpu.with_memory_space_constraint(x, pltpu.HBM) for x in (owner_map, median_bin, mad_bin, hit_mask, tiles)))
     snr, keys, excess = pl.pallas_call(
         functools.partial(compact_kernel, n),
         out_shape=[
@@ -312,6 +333,7 @@
         in_specs=[smem] + [vmem] * 3,
         out_specs=[vmem] * 3,
         scratch_shapes=[VMEM((n * CAP, BLOCK), F32), VMEM((n + 8, BLOCK), F32), VMEM((n + 8, BLOCK), F32)],
+        compiler_params=pltpu.CompilerParams(vmem_limit_bytes=16 * 1024 * 1024),
         name="compact",
     )(begins, rows, keys, excess)
     total = n * CAP

time: 129 us -> 125 us (0.969)
  Pallas kernels: 128 us -> 124 us
    pallas_call x1, Pallas kernels: 125 us -> 122 us  [per_device(): pl.pallas_call(functools.partial(exchange_kernel, n, coarse, drift, total...]
where the time goes in v3:
time: 125 us
  Pallas kernels  124 us (99%)
    pallas_call x1, Pallas kernels, per_device(): pl.pallas_call(functools.partial(exchange_kernel, n, coarse, drift, total...  122 us

profile of v3, /device:TPU:37, one launch (start us, length us, event | category | flops | bytes accessed | tf_op | source)
XLA Modules:
  0.0 124.8 jit_solution(6461436279440393230)
XLA Ops:
  0.6 122.0 %exchange.1 = (bf16[32,128,128]{2,1,0:T(8,128)(2,1)S(1)}, f32[32,128]{1,0:T(8,128)S(1)}, f32[32,128]{1,0:T(8,128)S(1)}, s32[8,32]{1,0:T(8,128)S(1)}) custom-call(s32[32]{0:T(128)} %owner_hbm.1, s32[32]{0:T(128)} %median_hbm.1, s32[32]{0:T(128)} %mad_hbm.1, s32[32,256]{1,0:T(8,128)} %marks_hbm.1, bf16[4,256,8,128]{3,2,1,0:T(8,128)(2,1)} %bitcast.6), custom_call_target="tpu_custom_call" | custom-call | tf_op jit(solution)/shard_map/exchange/pallas_call | solution.py:301
  122.7 2.1 %compact.1 = (bf16[4096,128]{1,0:T(8,128)(2,1)}, s32[32,128]{1,0:T(8,128)}, f32[32,128]{1,0:T(8,128)}) custom-call(s32[8,32]{1,0:T(8,128)S(1)} %get-tuple-element.10.begins, bf16[32,128,128]{2,1,0:T(8,128)(2,1)S(1)} %get-tuple-element.11.rows, f32[32,128]{1,0:T(8,128)S(1)} %get-tuple-element.12.keys, f32[32,128]{1,0:T(8,128)S(1)} %get-tuple-element.13.excess), custom_call_target="tpu_custom_call" | custom-call | tf_op jit(solution)/shard_map/compact/pallas_call | solution.py:326

commit v4 on v3

--- a/solution.py
+++ b/solution.py
@@ -28,7 +28,7 @@
     return lax.dot_general(a, b, (((1,), (1,)), ((), ())), preferred_element_type=F32)
 
 
-REACH = 4
+REACH = 2
 
 
 def exchange_kernel(
@@ -59,10 +59,10 @@
         large.append(pltpu.make_async_copy(spec_hbm.at[:, part], spec.at[:, part], spec_sems.at[g]))
     for copy in small + large:
         copy.start()
-    pl.semaphore_signal(barrier, inc=1, device_id={"sub": 1 - half}, device_id_type=MESH)
-    for d in range(1, REACH + 1):
+    for d in range(REACH, 0, -1):
         for to in (me + d, me + n - d):
             pl.semaphore_signal(barrier, inc=1, device_id={"freq": to % n}, device_id_type=MESH)
+    pl.semaphore_signal(barrier, inc=1, device_id={"sub": 1 - half}, device_id_type=MESH)
 
     for copy in small:
         copy.wait()
@@ -91,10 +91,9 @@
     rank[...] = jnp.where(set_here > 0, ranks, -1.0)
     filled[...] = jnp.broadcast_to(jnp.sum(set_here, axis=1, keepdims=True), filled.shape)
 
-    early = [m for m in (2, 4, 3) if m <= REACH and m < far]
-    middle = [m for m in (6,) if REACH < m <= 2 * REACH and m < far]
+    early = [m for m in (2, 1, 4, 3) if m <= 2 * REACH and m < far]
+    middle = [m for m in (6, 5) if 2 * REACH < m <= 3 * REACH and m < far]
     late = [m for m in range(far - 1, 0, -1) if m not in early + middle]
-    run = next((k for k in range(1, len(late)) if late[k] != late[0] - k), len(late))
 
     def ways(ms):
         return [d for m in ms for d in (m, n - m)]
@@ -138,15 +137,20 @@
         row_copy(d).start()
 
     def each_late(act):
-        def body(k, carry):
-            act(late[0] - k)
-            act(n - late[0] + k)
-            return carry
         act(far)
-        if late:
-            lax.fori_loop(0, run, body, 0)
-        for d in ways(late[run:]):
-            act(d)
+        at = 0
+        while at < len(late):
+            size = next((k for k in range(1, len(late) - at) if late[at + k] != late[at] - k), len(late) - at)
+            if size > 2:
+                def body(k, carry, top=late[at]):
+                    act(top - k)
+                    act(n - top + k)
+                    return carry
+                lax.fori_loop(0, size, body, 0)
+            else:
+                for d in ways(late[at : at + size]):
+                    act(d)
+            at += size
 
     def tell(k):
         if k < rounds:
@@ -173,7 +177,10 @@
         send_codes[d] = codes
     pl.semaphore_wait(barrier, 2 * REACH + 1)
     tell(0)
-    for d in ways(early):
+    for d in ways([m for m in early if m <= REACH]):
+        send(d)
+    hear(0)
+    for d in ways([m for m in early if m > REACH]):
         send(d)
 
     def stats(c, carry):
@@ -193,14 +200,17 @@
             mine[k, pl.ds(c, 1), :] = jnp.sum(jnp.sum(each, axis=(0, 1)), axis=0, keepdims=True)
         return carry
 
-    lax.fori_loop(0, coarse, stats, 0, unroll=2)
-    hear(0)
+    lax.fori_loop(0, coarse // 2, stats, 0, unroll=2)
+    hear(1)
+    lax.fori_loop(coarse // 2, coarse, stats, 0, unroll=2)
+    hear(2)
     share = pltpu.make_async_remote_copy(
         src_ref=mine, dst_ref=theirs, send_sem=stat_sems.at[0], recv_sem=stat_sems.at[1],
         device_id={"sub": 1 - half}, device_id_type=MESH,
     )
     share.start()
     share.wait()
+    hear(3)
     total = [jnp.sum(mine[k] + theirs[k], axis=1, keepdims=True) for k in range(3)]
     floor = jnp.maximum(total[0], 1.0)
     mean[...] = mean[...] + total[1] / floor
@@ -213,9 +223,9 @@
         norm_copy(d).start()
     for d in ways(middle):
         send(d)
-    hear(1)
+    hear(4)
     each_late(pack)
-    for k in range(2, rounds):
+    for k in range(5, rounds):
         hear(k)
     each_late(lambda d: code_copy(d).start())
     each_late(lambda d: row_copy(d).start())
@@ -269,23 +279,40 @@
     each_late(rows_in)
 
 
-def compact_kernel(n, begins, rows, keys, excess, snr_out, keys_out, excess_out, wide, key_rows, excess_rows):
+def compact_kernel(
+    n, begins_vmem, rows, keys, excess, snr_out, keys_out, excess_out, wide, narrow, key_rows, excess_rows, begins, sems
+):
+    fetch = pltpu.make_async_copy(begins_vmem, begins, sems.at[0])
+    fetch.start()
     wide[...] = jnp.zeros_like(wide)
     key_rows[...] = jnp.full_like(key_rows, -1.0)
     excess_rows[...] = jnp.zeros_like(excess_rows)
     lane = lax.broadcasted_iota(jnp.int32, (1, BLOCK), 1)
+    fetch.wait()
     for s in range(n):
-        begin = begins[0, s]
-        wide[pl.ds(begin, CAP), :] = rows[s].astype(F32)
-        row, shift = begin // BLOCK, begin % BLOCK
+        wide[pl.ds(begins[0, s], CAP), :] = rows[s].astype(F32)
+    parts = sems.shape[0] - 1
+    size = n * CAP // parts
+    writes = []
+    for k in range(parts):
+        part = pl.ds(k * size, size)
+        narrow[part, :] = wide[part, :].astype(BF16)
+        writes.append(pltpu.make_async_copy(narrow.at[part, :], snr_out.at[part, :], sems.at[k + 1]))
+        if k:
+            writes[k - 1].start()
+    for s in range(n):
+        row, shift = lax.div(begins[0, s], BLOCK), lax.rem(begins[0, s], BLOCK)
         for source, target, empty in ((keys, key_rows, -1.0), (excess, excess_rows, 0.0)):
             turned = pltpu.roll(source[pl.ds(s, 1), :], shift, 1)
             here, after = pl.ds(row, 1), pl.ds(row + 1, 1)
             target[here, :] = jnp.where(lane >= shift, turned, target[here, :])
             target[after, :] = jnp.where(lane < shift, turned, empty)
-    snr_out[...] = wide[...].astype(BF16)
+        if s == 0:
+            writes[-1].start()
     keys_out[...] = key_rows[0:n, :].astype(jnp.int32)
     excess_out[...] = excess_rows[0:n, :]
+    for write in writes:
+        write.wait()
 
 
 def per_device(spectrum, hit_mask, owner_map, median_bin, mad_bin):
@@ -294,7 +321,7 @@
     n = lax.axis_size("freq")
     total_drift = drift * lax.axis_size("sub")
     width = PER * drift
-    vmem, smem = pl.BlockSpec(memory_space=VMEM), pl.BlockSpec(memory_space=SMEM)
+    vmem = pl.BlockSpec(memory_space=VMEM)
     tiles = spectrum.reshape(drift // 8, 8, coarse * PER, BLOCK).transpose(0, 2, 1, 3)
     table, line = VMEM((coarse, BLOCK), F32), VMEM((n, 1, CAP), F32)
     dma = pltpu.SemaphoreType.DMA
@@ -330,9 +357,12 @@
             jax.ShapeDtypeStruct((n, BLOCK), jnp.int32),
             jax.ShapeDtypeStruct((n, BLOCK), F32),
         ],
-        in_specs=[smem] + [vmem] * 3,
-        out_specs=[vmem] * 3,
-        scratch_shapes=[VMEM((n * CAP, BLOCK), F32), VMEM((n + 8, BLOCK), F32), VMEM((n + 8, BLOCK), F32)],
+        in_specs=[vmem] * 4,
+        out_specs=[pl.BlockSpec(memory_space=pltpu.HBM), vmem, vmem],
+        scratch_shapes=[
+            VMEM((n * CAP, BLOCK), F32), VMEM((n * CAP, BLOCK), BF16),
+            VMEM((n + 8, BLOCK), F32), VMEM((n + 8, BLOCK), F32), SMEM((8, n), jnp.int32), dma((5,)),
+        ],
         compiler_params=pltpu.CompilerParams(vmem_limit_bytes=16 * 1024 * 1024),
         name="compact",
     )(begins, rows, keys, excess)

time: 125 us -> 125 us (level)
  no operation moved by 1% of the time
where the time goes in v4:
time: 125 us
  Pallas kernels  124 us (99%)
    pallas_call x1, Pallas kernels, per_device(): pl.pallas_call(functools.partial(exchange_kernel, n, coarse, drift, total...  121 us
    pallas_call x1, Pallas kernels, per_device(): pl.pallas_call(functools.partial(compact_kernel, n), out_shape=[jax.Shape...  2.61 us

profile of v4, /device:TPU:37, one launch (start us, length us, event | category | flops | bytes accessed | tf_op | source)
XLA Modules:
  0.0 124.7 jit_solution(9532689896368919943)
XLA Ops:
  0.6 121.4 %exchange.1 = (bf16[32,128,128]{2,1,0:T(8,128)(2,1)S(1)}, f32[32,128]{1,0:T(8,128)S(1)}, f32[32,128]{1,0:T(8,128)S(1)}, s32[8,32]{1,0:T(8,128)S(1)}) custom-call(s32[32]{0:T(128)} %owner_hbm.1, s32[32]{0:T(128)} %median_hbm.1, s32[32]{0:T(128)} %mad_hbm.1, s32[32,256]{1,0:T(8,128)} %marks_hbm.1, bf16[4,256,8,128]{3,2,1,0:T(8,128)(2,1)} %bitcast.6), custom_call_target="tpu_custom_call" | custom-call | tf_op jit(solution)/shard_map/exchange/pallas_call | solution.py:328
  122.1 2.6 %compact.1 = (bf16[4096,128]{1,0:T(8,128)(2,1)}, s32[32,128]{1,0:T(8,128)}, f32[32,128]{1,0:T(8,128)}) custom-call(s32[8,32]{1,0:T(8,128)S(1)} %get-tuple-element.10.begins_vmem, bf16[32,128,128]{2,1,0:T(8,128)(2,1)S(1)} %get-tuple-element.11.rows, f32[32,128]{1,0:T(8,128)S(1)} %get-tuple-element.12.keys, f32[32,128]{1,0:T(8,128)S(1)} %get-tuple-element.13.excess), custom_call_target="tpu_custom_call" | custom-call | tf_op jit(solution)/shard_map/compact/pallas_call | solution.py:353

commit v5 on v4

--- a/solution.py
+++ b/solution.py
@@ -28,7 +28,7 @@
     return lax.dot_general(a, b, (((1,), (1,)), ((), ())), preferred_element_type=F32)
 
 
-REACH = 2
+REACH = 4
 
 
 def exchange_kernel(
@@ -59,10 +59,10 @@
         large.append(pltpu.make_async_copy(spec_hbm.at[:, part], spec.at[:, part], spec_sems.at[g]))
     for copy in small + large:
         copy.start()
-    for d in range(REACH, 0, -1):
+    pl.semaphore_signal(barrier, inc=1, device_id={"sub": 1 - half}, device_id_type=MESH)
+    for d in range(1, REACH + 1):
         for to in (me + d, me + n - d):
             pl.semaphore_signal(barrier, inc=1, device_id={"freq": to % n}, device_id_type=MESH)
-    pl.semaphore_signal(barrier, inc=1, device_id={"sub": 1 - half}, device_id_type=MESH)
 
     for copy in small:
         copy.wait()
@@ -91,8 +91,8 @@
     rank[...] = jnp.where(set_here > 0, ranks, -1.0)
     filled[...] = jnp.broadcast_to(jnp.sum(set_here, axis=1, keepdims=True), filled.shape)
 
-    early = [m for m in (2, 1, 4, 3) if m <= 2 * REACH and m < far]
-    middle = [m for m in (6, 5) if 2 * REACH < m <= 3 * REACH and m < far]
+    early = [m for m in (4, 3, 2, 1) if m <= REACH and m < far]
+    middle = [m for m in (6, 5) if REACH < m <= 2 * REACH and m < far]
     late = [m for m in range(far - 1, 0, -1) if m not in early + middle]
 
     def ways(ms):
@@ -177,10 +177,7 @@
         send_codes[d] = codes
     pl.semaphore_wait(barrier, 2 * REACH + 1)
     tell(0)
-    for d in ways([m for m in early if m <= REACH]):
-        send(d)
-    hear(0)
-    for d in ways([m for m in early if m > REACH]):
+    for d in ways(early):
         send(d)
 
     def stats(c, carry):
@@ -200,17 +197,14 @@
             mine[k, pl.ds(c, 1), :] = jnp.sum(jnp.sum(each, axis=(0, 1)), axis=0, keepdims=True)
         return carry
 
-    lax.fori_loop(0, coarse // 2, stats, 0, unroll=2)
-    hear(1)
-    lax.fori_loop(coarse // 2, coarse, stats, 0, unroll=2)
-    hear(2)
+    lax.fori_loop(0, coarse, stats, 0, unroll=2)
+    hear(0)
     share = pltpu.make_async_remote_copy(
         src_ref=mine, dst_ref=theirs, send_sem=stat_sems.at[0], recv_sem=stat_sems.at[1],
         device_id={"sub": 1 - half}, device_id_type=MESH,
     )
     share.start()
     share.wait()
-    hear(3)
     total = [jnp.sum(mine[k] + theirs[k], axis=1, keepdims=True) for k in range(3)]
     floor = jnp.maximum(total[0], 1.0)
     mean[...] = mean[...] + total[1] / floor
@@ -223,9 +217,9 @@
         norm_copy(d).start()
     for d in ways(middle):
         send(d)
-    hear(4)
+    hear(1)
     each_late(pack)
-    for k in range(5, rounds):
+    for k in range(2, rounds):
         hear(k)
     each_late(lambda d: code_copy(d).start())
     each_late(lambda d: row_copy(d).start())
@@ -280,7 +274,7 @@
 
 
 def compact_kernel(
-    n, begins_vmem, rows, keys, excess, snr_out, keys_out, excess_out, wide, narrow, key_rows, excess_rows, begins, sems
+    n, begins_vmem, rows, keys, excess, snr_out, keys_out, excess_out, wide, narrow, key_rows, excess_rows, key_ints, begins, sems
 ):
     fetch = pltpu.make_async_copy(begins_vmem, begins, sems.at[0])
     fetch.start()
@@ -290,27 +284,31 @@
     lane = lax.broadcasted_iota(jnp.int32, (1, BLOCK), 1)
     fetch.wait()
     for s in range(n):
-        wide[pl.ds(begins[0, s], CAP), :] = rows[s].astype(F32)
-    parts = sems.shape[0] - 1
-    size = n * CAP // parts
-    writes = []
-    for k in range(parts):
-        part = pl.ds(k * size, size)
-        narrow[part, :] = wide[part, :].astype(BF16)
-        writes.append(pltpu.make_async_copy(narrow.at[part, :], snr_out.at[part, :], sems.at[k + 1]))
-        if k:
-            writes[k - 1].start()
-    for s in range(n):
-        row, shift = lax.div(begins[0, s], BLOCK), lax.rem(begins[0, s], BLOCK)
+        begin = begins[0, s]
+        wide[pl.ds(begin, CAP), :] = rows[s].astype(F32)
+        row, shift = lax.div(begin, BLOCK), lax.rem(begin, BLOCK)
         for source, target, empty in ((keys, key_rows, -1.0), (excess, excess_rows, 0.0)):
             turned = pltpu.roll(source[pl.ds(s, 1), :], shift, 1)
             here, after = pl.ds(row, 1), pl.ds(row + 1, 1)
             target[here, :] = jnp.where(lane >= shift, turned, target[here, :])
             target[after, :] = jnp.where(lane < shift, turned, empty)
-        if s == 0:
-            writes[-1].start()
-    keys_out[...] = key_rows[0:n, :].astype(jnp.int32)
-    excess_out[...] = excess_rows[0:n, :]
+    key_ints[...] = key_rows[0:n, :].astype(jnp.int32)
+    parts = sems.shape[0] - 3
+    size = n * CAP // parts
+    writes = [
+        pltpu.make_async_copy(key_ints, keys_out, sems.at[parts + 1]),
+        pltpu.make_async_copy(excess_rows.at[pl.ds(0, n), :], excess_out, sems.at[parts + 2]),
+    ]
+    for k in range(parts):
+        part = pl.ds(k * size, size)
+        narrow[part, :] = wide[part, :].astype(BF16)
+        writes.append(pltpu.make_async_copy(narrow.at[part, :], snr_out.at[part, :], sems.at[k + 1]))
+        if k == 1:
+            writes[0].start()
+            writes[1].start()
+        if k:
+            writes[k + 1].start()
+    writes[-1].start()
     for write in writes:
         write.wait()
 
@@ -358,10 +356,11 @@
             jax.ShapeDtypeStruct((n, BLOCK), F32),
         ],
         in_specs=[vmem] * 4,
-        out_specs=[pl.BlockSpec(memory_space=pltpu.HBM), vmem, vmem],
+        out_specs=[pl.BlockSpec(memory_space=pltpu.HBM)] * 3,
         scratch_shapes=[
             VMEM((n * CAP, BLOCK), F32), VMEM((n * CAP, BLOCK), BF16),
-            VMEM((n + 8, BLOCK), F32), VMEM((n + 8, BLOCK), F32), SMEM((8, n), jnp.int32), dma((5,)),
+            VMEM((n + 8, BLOCK), F32), VMEM((n + 8, BLOCK), F32), VMEM((n, BLOCK), jnp.int32),
+            SMEM((8, n), jnp.int32), dma((7,)),
         ],
         compiler_params=pltpu.CompilerParams(vmem_limit_bytes=16 * 1024 * 1024),
         name="compact",

time: 125 us -> 124 us (level)
  no operation moved by 1% of the time
where the time goes in v5:
time: 124 us; the launch traced here: 123 us
  Pallas kernels  123 us (99%)
    pallas_call x1, Pallas kernels, per_device(): pl.pallas_call(functools.partial(exchange_kernel, n, coarse, drift, total...  121 us

profile of v5, /device:TPU:37, one launch (start us, length us, event | category | flops | bytes accessed | tf_op | source)
XLA Modules:
  0.0 123.4 jit_solution(9789232497130038180)
XLA Ops:
  0.6 120.8 %exchange.1 = (bf16[32,128,128]{2,1,0:T(8,128)(2,1)S(1)}, f32[32,128]{1,0:T(8,128)S(1)}, f32[32,128]{1,0:T(8,128)S(1)}, s32[8,32]{1,0:T(8,128)S(1)}) custom-call(s32[32]{0:T(128)} %owner_hbm.1, s32[32]{0:T(128)} %median_hbm.1, s32[32]{0:T(128)} %mad_hbm.1, s32[32,256]{1,0:T(8,128)} %marks_hbm.1, bf16[4,256,8,128]{3,2,1,0:T(8,128)(2,1)} %bitcast.6), custom_call_target="tpu_custom_call" | custom-call | tf_op jit(solution)/shard_map/exchange/pallas_call | solution.py:326
  121.4 2.0 %compact.1 = (bf16[4096,128]{1,0:T(8,128)(2,1)}, s32[32,128]{1,0:T(8,128)}, f32[32,128]{1,0:T(8,128)}) custom-call(s32[8,32]{1,0:T(8,128)S(1)} %get-tuple-element.10.begins_vmem, bf16[32,128,128]{2,1,0:T(8,128)(2,1)S(1)} %get-tuple-element.11.rows, f32[32,128]{1,0:T(8,128)S(1)} %get-tuple-element.12.keys, f32[32,128]{1,0:T(8,128)S(1)} %get-tuple-element.13.excess), custom_call_target="tpu_custom_call" | custom-call | tf_op jit(solution)/shard_map/compact/pallas_call | solution.py:351

commit v6 on v5

--- a/solution.py
+++ b/solution.py
@@ -237,7 +237,8 @@
     def take_rows(s):
         over = jnp.maximum(rows[s].astype(F32) - THRESH, 0.0)
         coarse_part = over.astype(BF16)
-        fine_part = (over - coarse_part.astype(F32)).astype(BF16)
+        left = over - coarse_part.astype(F32)
+        fine_part = jnp.where(left == left, left, 0.0).astype(BF16)
         excess[pl.ds(s, 1), :] = (dot_nt(ones, coarse_part) + dot_nt(ones, fine_part))[0:1]
 
     def codes_in(d):

time: 124 us -> 124 us (level)
  no operation moved by 1% of the time
where the time goes in v6:
time: 124 us; the launch traced here: 123 us
  Pallas kernels  123 us (99%)
    pallas_call x1, Pallas kernels, per_device(): pl.pallas_call(functools.partial(exchange_kernel, n, coarse, drift, total...  121 us

profile of v6, /device:TPU:37, one launch (start us, length us, event | category | flops | bytes accessed | tf_op | source)
XLA Modules:
  0.0 123.4 jit_solution(6379060455935320096)
XLA Ops:
  0.6 120.8 %exchange.1 = (bf16[32,128,128]{2,1,0:T(8,128)(2,1)S(1)}, f32[32,128]{1,0:T(8,128)S(1)}, f32[32,128]{1,0:T(8,128)S(1)}, s32[8,32]{1,0:T(8,128)S(1)}) custom-call(s32[32]{0:T(128)} %owner_hbm.1, s32[32]{0:T(128)} %median_hbm.1, s32[32]{0:T(128)} %mad_hbm.1, s32[32,256]{1,0:T(8,128)} %marks_hbm.1, bf16[4,256,8,128]{3,2,1,0:T(8,128)(2,1)} %bitcast.6), custom_call_target="tpu_custom_call" | custom-call | tf_op jit(solution)/shard_map/exchange/pallas_call | solution.py:327
  121.4 2.0 %compact.1 = (bf16[4096,128]{1,0:T(8,128)(2,1)}, s32[32,128]{1,0:T(8,128)}, f32[32,128]{1,0:T(8,128)}) custom-call(s32[8,32]{1,0:T(8,128)S(1)} %get-tuple-element.10.begins_vmem, bf16[32,128,128]{2,1,0:T(8,128)(2,1)S(1)} %get-tuple-element.11.rows, f32[32,128]{1,0:T(8,128)S(1)} %get-tuple-element.12.keys, f32[32,128]{1,0:T(8,128)S(1)} %get-tuple-element.13.excess), custom_call_target="tpu_custom_call" | custom-call | tf_op jit(solution)/shard_map/compact/pallas_call | solution.py:352
